TPU v7x, 32 devices: a whole 2x2x4 slice. The times are simulated.
32 devices in a mesh: segment: 4 (over y, core), dp: 8 (over z, x).
Axes of the slice: x: 2, y: 2, z: 4, core: 2. Of those that a mesh axis runs over, the one named last changes fastest.
Arguments:
- token_ids: int32 [1024], P('dp'), may hold values from 0 to 38015, as said below
- table: bfloat16 [4752, 28672], P('segment', 'dp'), may hold values from -6 to 6
- out_grad: bfloat16 [1024, 3584], P('dp', 'segment'), may hold values from -6 to 6
Outputs:
- embedded: bfloat16 [1024, 3584], P('dp')
- table_grad: bfloat16 [4752, 28672], P('segment', 'dp')
Inputs may be any that keep to these rules, and one draw needn't show every extreme that they name: `token_ids`: in the 128 tokens of each data group, at most 16 ids lie in one segment's slice of 9504 rows with one residue modulo 8; in every data group some segment and residue has exactly 16.
All inputs are finite; a program needn't handle non-finite values.
Results may differ from a plain program's by a relative error of at most 0.001.
Values may be sent and summed in bfloat16 or wider, within the bound.
A program may use at most 64 MiB of HBM per device.

v0:
```python
import jax
import jax.numpy as jnp
from jax import lax
from jax.sharding import PartitionSpec as P

D = 3584
PACK = 8


def body(token_ids, table, out_grad):
    lines = table.shape[0]
    width = table.shape[1]
    groups = lax.axis_size("dp")
    tok_rows = token_ids.shape[0]
    quarters = D // width
    slot = lax.axis_index("dp") // quarters
    first = lax.axis_index("segment") * lines * PACK
    every_id = lax.all_gather(token_ids, "dp", axis=0, tiled=True)
    local = every_id - first
    in_section = (local >= 0) & (local < lines * PACK)
    owned = in_section & (local % PACK == slot)
    line_idx = jnp.clip(local // PACK, 0, lines - 1)
    whole_grad = lax.all_gather(out_grad, "segment", axis=1, tiled=True)
    capacity = tok_rows // PACK
    owned_grid = owned.reshape(groups, tok_rows)
    rank = jnp.cumsum(owned_grid.astype(jnp.int32), axis=1) - 1
    place = jnp.where(owned_grid, rank, capacity)
    group_rows = jnp.broadcast_to(jnp.arange(groups, dtype=jnp.int32)[:, None], (groups, tok_rows))
    row_of = (
        jnp.zeros((groups, capacity), jnp.int32)
        .at[group_rows, place]
        .set(line_idx.reshape(groups, tok_rows), mode="drop")
    )
    filled = jnp.zeros((groups, capacity), jnp.bool_).at[group_rows, place].set(True, mode="drop")
    fetched = jnp.take(table, row_of.reshape(-1), axis=0).reshape(groups, capacity, width)
    fetched = jnp.where(filled[:, :, None], fetched, jnp.zeros((), jnp.bfloat16))
    arrived = lax.all_to_all(fetched, "dp", split_axis=0, concat_axis=0, tiled=True)
    my_local = token_ids - first
    my_in = (my_local >= 0) & (my_local < lines * PACK)
    my_slot = my_local % PACK
    slot_hits = (my_slot[:, None] == jnp.arange(PACK, dtype=jnp.int32)[None, :]) & my_in[:, None]
    slot_ranks = jnp.cumsum(slot_hits.astype(jnp.int32), axis=0) - 1
    my_rank = jnp.sum(jnp.where(slot_hits, slot_ranks, 0), axis=1)
    sources = my_slot[:, None] * quarters + jnp.arange(quarters, dtype=jnp.int32)[None, :]
    flat_index = jnp.clip(sources * capacity + my_rank[:, None], 0, groups * capacity - 1)
    gathered = jnp.take(
        arrived.reshape(groups * capacity, width), flat_index.reshape(-1), axis=0
    ).reshape(tok_rows, D)
    segment_part = jnp.where(my_in[:, None], gathered.astype(jnp.float32), 0.0)
    slot_place = jnp.where(my_in, my_slot, PACK)
    token_at = (
        jnp.zeros((PACK, capacity), jnp.int32)
        .at[slot_place, my_rank]
        .set(jnp.arange(tok_rows, dtype=jnp.int32), mode="drop")
    )
    valid = jnp.zeros((PACK, capacity), jnp.bool_).at[slot_place, my_rank].set(True, mode="drop")
    grad_pick = jnp.take(whole_grad, token_at.reshape(-1), axis=0).reshape(
        PACK, capacity, quarters, width
    )
    grad_pick = jnp.where(valid[:, :, None, None], grad_pick, jnp.zeros((), jnp.bfloat16))
    grad_send = grad_pick.transpose(0, 2, 1, 3).reshape(groups, capacity, width)
    returned = lax.all_to_all(grad_send, "dp", split_axis=0, concat_axis=0, tiled=True)
    target = jnp.where(filled, row_of, lines)
    accum = (
        jnp.zeros((lines, width), jnp.float32)
        .at[target.reshape(-1)]
        .add(returned.reshape(-1, width).astype(jnp.float32), mode="drop")
    )
    embedded = lax.psum(segment_part.astype(jnp.bfloat16), "segment")
    return (embedded, accum.astype(jnp.bfloat16))


def solution(mesh):
    placed = (P("dp"), P("segment", "dp"), P("dp", "segment"))
    return jax.shard_map(
        body,
        mesh=mesh,
        in_specs=placed,
        out_specs=(P("dp", None), P("segment", "dp")),
        check_vma=False,
    )
```

profile of v0, /device:TPU:0, one launch (start us, length us, event | category | flops | bytes accessed | tf_op | source)
XLA Modules:
  0.0 159.1 jit_solution(7434590179938538914)
XLA Ops:
  7.2 0.0 copy-start.1
  7.2 0.0 copy-start
  7.2 22.6 %all-gather = s32[8,1,128]{2,1,0:T(1,128)S(1)} all-gather(s32[1,1,128]{2,1,0:T(1,128)} %bitcast.39), channel_id=1, replica_groups=mesh['segment'=4,'dp'=8] {'dp'}, dimensions={0}, use_global_device_ids=true | all-gather | bytes 4608 | tf_op jit(solution)/shard_map/all_gather | solution.py:18
  29.8 0.3 copy.12
  30.1 0.3 copy.13
  30.4 23.6 %compare_select_fusion = s32[8,128,1]{2,0,1:T(8,128)S(1)} fusion(pred[8,128,1]{2,0,1:T(8,128)(4,1)S(1)} %copy.13, s32[8,128,1]{2,0,1:T(8,128)S(1)} %copy.12), kind=kOutput, calls=%fused_computation.12 | output fusion | flops 135168 | bytes 9216 | tf_op jit(solution)/shard_map/jit(cumsum)/reduce_window_sum | solution.py:26
  54.0 0.2 copy.14
  54.2 0.8 multiply_reduce_fusion
  55.0 0.1 copy.19
  55.1 0.7 and_reduce_fusion
  55.8 0.1 copy.18
  56.0 4.3 %scatter_custom_fusion.4 = s32[128]{0:T(128)S(1)} fusion(s32[1024]{0:T(1024)S(1)} %bitcast.40, s32[1024]{0:T(1024)S(1)} %fusion.6, s32[]{:T(128)} %constant.70.clone.1), kind=kCustom, calls=%fused_computation.66 | custom fusion | bytes 516
  60.3 0.1 reshape.189
  60.4 4.3 %scatter_custom_fusion.3 = pred[128]{0:T(512)(128)(4,1)S(1)} fusion(s32[1024]{0:T(1024)S(1)} %bitcast.41, pred[1024]{0:T(1024)(128)(4,1)S(1)} %broadcast.224, pred[]{:T(512)} %constant.71.clone.1), kind=kCustom, calls=%fused_computation.56 | custom fusion | bytes 129
  64.8 0.1 reshape.185
  64.9 6.6 %gather_fusion = bf16[128,3584]{1,0:T(8,128)(2,1)S(1)} fusion(bf16[1188,3584]{1,0:T(8,128)(2,1)} %param.6, s32[1024]{0:T(1024)S(1)} %pad_clamp_fusion.2), kind=kCustom, calls=%fused_computation.2 | custom fusion | bytes 1835520 | tf_op jit(solution)/shard_map/jit(_take)/gather | solution.py:35
  71.4 1.1 select_select_fusion
  72.6 3.6 %all-to-all-start = ((bf16[8,16,3584]{2,1,0:T(8,128)(2,1)}), bf16[8,16,3584]{2,1,0:T(8,128)(2,1)S(1)}, u32[]{:S(2)}, u32[]{:S(2)}) async-start(bf16[8,16,3584]{2,1,0:T(8,128)(2,1)} %select_select_fusion), calls=%async_computation | async-start | bytes 1835008 | tf_op jit(solution)/shard_map/all_to_all | solution.py:37
  76.1 0.0 copy-done.1
  76.2 0.1 fusion.4
  76.3 0.2 reduce_window_sum.23
  76.4 0.2 select_reduce_fusion
  76.7 6.4 %scatter_fusion.1 = s32[8,16]{1,0:T(8,128)S(1)} fusion(s32[8,16]{1,0:T(8,128)S(1)} %broadcast.169, s32[128]{0:T(128)S(1)} %fusion.18, s32[128]{0:T(128)S(1)} %iota.14), kind=kCustom, calls=%fused_computation.4 | custom fusion | bytes 2560 | tf_op jit(solution)/shard_map/scatter | solution.py:54
  83.0 0.1 reshape.180
  83.1 0.0 copy-done
  83.2 9.5 %all_gather.7 = bf16[128,3584]{1,0:T(8,128)(2,1)S(1)} all-gather(bf16[128,896]{1,0:T(8,128)(2,1)S(1)} %copy-done), channel_id=1, replica_groups=mesh['segment'=4,'dp'=8] {'segment'}, dimensions={1}, use_global_device_ids=true | all-gather | bytes 1146880 | tf_op jit(solution)/shard_map/all_gather | solution.py:23
  92.7 1.1 gather_fusion.2
  93.8 6.5 %scatter_fusion = pred[8,16]{1,0:T(8,128)(4,1)S(1)} fusion(pred[8,16]{1,0:T(8,128)(4,1)S(1)} %broadcast.166, s32[128]{0:T(128)S(1)} %fusion.18, pred[128]{0:T(512)(128)(4,1)S(1)} %broadcast.225), kind=kCustom, calls=%fused_computation.3 | custom fusion | bytes 1408 | tf_op jit(solution)/shard_map/scatter | solution.py:56
  100.3 0.2 broadcast_select_fusion
  100.5 1.1 broadcast_select_fusion.1
  101.5 0.0 all-to-all-done
  101.5 5.9 %all-to-all-start.1 = ((bf16[8,16,3584]{2,1,0:T(8,128)(2,1)}), bf16[8,16,3584]{2,1,0:T(8,128)(2,1)S(1)}, u32[]{:S(2)}, u32[]{:S(2)}) async-start(bf16[8,16,3584]{2,1,0:T(8,128)(2,1)} %broadcast_select_fusion.1), calls=%async_computation.1 | async-start | bytes 1835008 | tf_op jit(solution)/shard_map/all_to_all | solution.py:62
  107.5 0.0 all-reduce.2.cloned.1.call-start
  107.5 1.1 gather_fusion.1
  108.7 1.3 select_convert_fusion
  109.9 0.0 all-reduce.2.cloned.1.call-update
  110.0 0.1 reshape.179
  110.1 20.9 %all-to-all-done.1 = bf16[8,16,3584]{2,1,0:T(8,128)(2,1)S(1)} async-done(((bf16[8,16,3584]{2,1,0:T(8,128)(2,1)}), bf16[8,16,3584]{2,1,0:T(8,128)(2,1)S(1)}, u32[]{:S(2)}, u32[]{:S(2)}) %all-to-all-start.1) | async-done | bytes 917536 | tf_op jit(solution)/shard_map/all_to_all | solution.py:62
  130.9 10.0 %scatter_custom_fusion.2 = f32[1188,3584]{1,0:T(8,128)} fusion(s32[128]{0:T(128)S(1)} %fusion.16, f32[]{:T(128)} %constant.121.clone.1, bf16[128,3584]{1,0:T(8,128)(2,1)S(1)} %bitcast.35), kind=kCustom, calls=%fused_computation.8 | custom fusion | flops 917504 | bytes 17948676 | tf_op jit(solution)/shard_map/scatter-add | solution.py:67
  140.9 9.1 %convert_element_type.32 = bf16[1188,3584]{1,0:T(8,128)(2,1)} convert(f32[1188,3584]{1,0:T(8,128)} %scatter_custom_fusion.2) | non-fusion elementwise | flops 4257792 | bytes 25546752 | tf_op jit(solution)/shard_map/convert_element_type | solution.py:70
  150.1 0.0 all-reduce.2.cloned.1.call-done
  150.1 2.2 %copy.23 = bf16[128,3584]{1,0:T(8,128)(2,1)} copy(bf16[128,3584]{1,0:T(8,128)(2,1)} %all-reduce.2.cloned.1.call-done) | data formatting | bytes 1835008
  (24 shorter events, 0.2 us)
Async XLA Ops:
  7.2 69.0 %copy-start.1 = (s32[128]{0:T(128)S(1)}, s32[128]{0:T(128)}, u32[]{:S(2)}) copy-start(s32[128]{0:T(128)} %param.5) | copy-start | bytes 1540
  7.2 76.0 %copy-start = (bf16[128,896]{1,0:T(8,128)(2,1)S(1)}, bf16[128,896]{1,0:T(8,128)(2,1)}, u32[]{:S(2)}) copy-start(bf16[128,896]{1,0:T(8,128)(2,1)} %param.7) | copy-start | bytes 688132
  72.6 29.0 %all-to-all-start = ((bf16[8,16,3584]{2,1,0:T(8,128)(2,1)}), bf16[8,16,3584]{2,1,0:T(8,128)(2,1)S(1)}, u32[]{:S(2)}, u32[]{:S(2)}) async-start(bf16[8,16,3584]{2,1,0:T(8,128)(2,1)} %select_select_fusion), calls=%async_computation | async-start | bytes 1835008 | tf_op jit(solution)/shard_map/all_to_all | solution.py:37
  101.5 29.4 %all-to-all-start.1 = ((bf16[8,16,3584]{2,1,0:T(8,128)(2,1)}), bf16[8,16,3584]{2,1,0:T(8,128)(2,1)S(1)}, u32[]{:S(2)}, u32[]{:S(2)}) async-start(bf16[8,16,3584]{2,1,0:T(8,128)(2,1)} %broadcast_select_fusion.1), calls=%async_computation.1 | async-start | bytes 1835008 | tf_op jit(solution)/shard_map/all_to_all | solution.py:62
  107.5 42.6 %all-reduce.2.cloned.1.call-start = ((), (), s32[]{:S(2)}) async-start(), calls=%async_computation.2 | async-start | bytes 1835008 | tf_op jit(solution)/shard_map/psum | solution.py:69
Sparse Core Ops, SparseCore 0:
  111.2 36.2 all-reduce.1
where the time goes:
time: 159 us
  other arithmetic  48.5 us (31%)
  local copies, waits for them, and re-layouts  33.8 us (21%)
  blocking collectives  32.1 us (20%)
  waiting for transfers between devices  20.9 us (13%)
  between operations  14.3 us (9%)
  starting transfers between devices  9.52 us (6%)
    another operation x1, other arithmetic, body(): rank = jnp.cumsum(owned_grid.astype(jnp.int32), axis=1) - 1  23.6 us
    all_gather x1, blocking collectives, body(): every_id = lax.all_gather(token_ids, 'dp', axis=0, tiled=True)  22.6 us
    all_to_all x1, waiting for transfers between devices, body(): lax.all_to_all(grad_send, 'dp', split_axis=0, concat_axis=0, tiled=True)  20.9 us
    unnamed x11, local copies, waits for them, and re-layouts  11.1 us
    scatter-add x1, other arithmetic, body(): accum = jnp.zeros((lines, width), jnp.float32).at[target.reshape(-1)].add...  10 us
    all_gather x1, blocking collectives, body(): whole_grad = lax.all_gather(out_grad, 'segment', axis=1, tiled=True)  9.52 us
    convert_element_type x1, other arithmetic, body(): return (embedded, accum.astype(jnp.bfloat16))  9.14 us
    gather x1, local copies, waits for them, and re-layouts, body(): jnp.take(table, row_of.reshape(-1), axis=0).reshape(groups, capacity, width)  6.55 us
  transfers between devices with their start and end apart: 3, of which 1 were waited for; matrix products, arithmetic and copies ran while one was open for 24% of the time, Pallas kernels for 0%

commit v1 on v0

--- a/solution.py
+++ b/solution.py
@@ -5,6 +5,24 @@
 
 D = 3584
 PACK = 8
+
+
+def collect(value, axis, dim):
+    ways, here, step = (lax.axis_size(axis), lax.axis_index(axis), value.shape[dim])
+    shape = [n * ways if d == dim else n for d, n in enumerate(value.shape)]
+    full = lax.dynamic_update_slice_in_dim(
+        jnp.zeros(shape, value.dtype), value, here * step, axis=dim
+    )
+    going_up = going_down = value
+    for far in range(1, ways // 2 + 1):
+        going_up = lax.ppermute(going_up, axis, [(d, (d + 1) % ways) for d in range(ways)])
+        full = lax.dynamic_update_slice_in_dim(full, going_up, (here - far) % ways * step, axis=dim)
+        if 2 * far < ways:
+            going_down = lax.ppermute(going_down, axis, [(d, (d - 1) % ways) for d in range(ways)])
+            full = lax.dynamic_update_slice_in_dim(
+                full, going_down, (here + far) % ways * step, axis=dim
+            )
+    return full
 
 
 def body(token_ids, table, out_grad):
@@ -15,7 +33,7 @@
     quarters = D // width
     slot = lax.axis_index("dp") // quarters
     first = lax.axis_index("segment") * lines * PACK
-    every_id = lax.all_gather(token_ids, "dp", axis=0, tiled=True)
+    every_id = collect(token_ids, "dp", 0)
     local = every_id - first
     in_section = (local >= 0) & (local < lines * PACK)
     owned = in_section & (local % PACK == slot)

time: 159 us -> 177 us (1.11)
  blocking collectives: 32.1 us -> 9.68 us
  waiting for transfers between devices: 20.9 us -> 42.3 us
  starting transfers between devices: 9.52 us -> 25.2 us
  local copies, waits for them, and re-layouts: 33.8 us -> 36.3 us
    all_gather x1 -> x0, blocking collectives: 22.6 us -> none  [body(): every_id = lax.all_gather(token_ids, 'dp', axis=0, tiled=True)]
    all_to_all x1, waiting for transfers between devices: 0.01 us -> 20.5 us  [body(): lax.all_to_all(fetched, 'dp', split_axis=0, concat_axis=0, tiled=True)]
    ppermute x0 -> x7, starting transfers between devices: none -> 15.6 us  [the longest x3 12.6 us: collect(): lax.ppermute(going_down, axis, [(d, (d - 1) % ways) for d in range(ways)])]
    all_to_all x1, starting transfers between devices: 3.55 us -> 6 us  [body(): lax.all_to_all(fetched, 'dp', split_axis=0, concat_axis=0, tiled=True)]
    all_to_all x1, starting transfers between devices: 5.93 us -> 3.55 us  [body(): lax.all_to_all(grad_send, 'dp', split_axis=0, concat_axis=0, tiled=True)]
    dynamic_update_slice x0 -> x8, local copies, waits for them, and re-layouts: none -> 2.31 us  [the longest x4 0.86 us: collect(): lax.dynamic_update_slice_in_dim(full, going_up, (here - far) % ways * ste...]
    unnamed x11 -> x13, local copies, waits for them, and re-layouts: 11.1 us -> 11.3 us
  transfers between devices with their start and end apart: 3 -> 10, of which waited for: 1 -> 3; matrix products, arithmetic and copies ran while one was open for 24% -> 24% of each run, Pallas kernels for 0% -> 0%
where the time goes in v1:
time: 177 us
  other arithmetic  49 us (28%)
  waiting for transfers between devices  42.3 us (24%)
  local copies, waits for them, and re-layouts  36.3 us (21%)
  starting transfers between devices  25.2 us (14%)
  between operations  14.3 us (8%)
  blocking collectives  9.68 us (5%)
    another operation x1, other arithmetic, body(): rank = jnp.cumsum(owned_grid.astype(jnp.int32), axis=1) - 1  23.3 us
    all_to_all x1, waiting for transfers between devices, body(): lax.all_to_all(fetched, 'dp', split_axis=0, concat_axis=0, tiled=True)  20.5 us
    all_to_all x1, waiting for transfers between devices, body(): lax.all_to_all(grad_send, 'dp', split_axis=0, concat_axis=0, tiled=True)  20.3 us
    ppermute x3, starting transfers between devices, collect(): lax.ppermute(going_down, axis, [(d, (d - 1) % ways) for d in range(ways)])  12.6 us
    unnamed x13, local copies, waits for them, and re-layouts  11.3 us
    scatter-add x1, other arithmetic, body(): accum = jnp.zeros((lines, width), jnp.float32).at[target.reshape(-1)].add...  10 us
    all_gather x1, blocking collectives, body(): whole_grad = lax.all_gather(out_grad, 'segment', axis=1, tiled=True)  9.68 us
    convert_element_type x1, other arithmetic, body(): return (embedded, accum.astype(jnp.bfloat16))  9.14 us
  transfers between devices with their start and end apart: 10, of which 3 were waited for; matrix products, arithmetic and copies ran while one was open for 24% of the time, Pallas kernels for 0%

profile of v1, /device:TPU:0, one launch (start us, length us, event | category | flops | bytes accessed | tf_op | source)
XLA Modules:
  0.0 176.8 jit_solution(16571594506045374793)
XLA Ops:
  7.2 0.0 copy-start.2
  7.2 0.0 copy-start.1
  7.2 3.0 %collective-permute-start = (s32[128]{0:T(128)}, s32[128]{0:T(128)S(1)}, u32[]{:S(2)}, u32[]{:S(2)}) collective-permute-start(s32[128]{0:T(128)} %param.5), channel_id=1, source_target_pairs={{0,1},{1,2},{2,3},{3,4},{4,5},{5,6},{6,7},{7,0},{8,9},{9,10},{10,1... | collective-permute-start | bytes 1544 | tf_op jit(solution)/shard_map/ppermute | solution.py:18
  10.2 3.1 %collective-permute-start.1 = (s32[128]{0:T(128)}, s32[128]{0:T(128)S(1)}, u32[]{:S(2)}, u32[]{:S(2)}) collective-permute-start(s32[128]{0:T(128)} %param.5), channel_id=1, source_target_pairs={{0,7},{1,0},{2,1},{3,2},{4,3},{5,4},{6,5},{7,6},{8,15},{9,8},{10,9... | collective-permute-start | bytes 1544 | tf_op jit(solution)/shard_map/ppermute | solution.py:21
  13.3 0.7 compare_and_fusion.3
  14.0 0.7 and_select_fusion
  14.7 0.1 fusion.4
  14.8 0.2 reduce_window_sum.23
  15.0 0.2 select_reduce_fusion
  15.1 0.7 fusion.18
  15.8 6.4 %scatter_fusion.1 = s32[8,16]{1,0:T(8,128)S(1)} fusion(s32[8,16]{1,0:T(8,128)S(1)} %broadcast.180, s32[128]{0:T(128)S(1)} %fusion.18, s32[128]{0:T(128)S(1)} %iota.14), kind=kCustom, calls=%fused_computation.4 | custom fusion | bytes 2560 | tf_op jit(solution)/shard_map/scatter | solution.py:72
  22.2 0.1 reshape.180
  22.3 9.7 %all_gather.3 = bf16[128,3584]{1,0:T(8,128)(2,1)S(1)} all-gather(bf16[128,896]{1,0:T(8,128)(2,1)} %param.7), channel_id=1, replica_groups=mesh['segment'=4,'dp'=8] {'segment'}, dimensions={1}, use_global_device_ids=true | all-gather | bytes 1146880 | tf_op jit(solution)/shard_map/all_gather | solution.py:41
  32.0 0.0 collective-permute-done
  32.0 0.0 collective-permute-start.2
  32.0 0.0 collective-permute-done.1
  32.0 4.7 %collective-permute-start.3 = (s32[128]{0:T(128)S(1)}, s32[128]{0:T(128)S(1)}, u32[]{:S(2)}, u32[]{:S(2)}) collective-permute-start(s32[128]{0:T(128)S(1)} %collective-permute-done.1), channel_id=1, source_target_pairs={{0,7},{1,0},{2,1},{3,2},{4,3},{5,4},{6,5},{7,6},{8,15},{9,8},{10,9... | collective-permute-start | bytes 1544 | tf_op jit(solution)/shard_map/ppermute | solution.py:21
  36.7 1.5 collective-permute-done.2
  38.3 0.0 collective-permute-start.4
  38.3 0.8 dynamic_update_slice.24
  39.1 1.1 gather_fusion.2
  40.2 0.0 collective-permute-done.3
  40.2 4.8 %collective-permute-start.5 = (s32[128]{0:T(128)S(1)}, s32[128]{0:T(128)S(1)}, u32[]{:S(2)}, u32[]{:S(2)}) collective-permute-start(s32[128]{0:T(128)S(1)} %collective-permute-done.3), channel_id=1, source_target_pairs={{0,7},{1,0},{2,1},{3,2},{4,3},{5,4},{6,5},{7,6},{8,15},{9,8},{10,9... | collective-permute-start | bytes 1544 | tf_op jit(solution)/shard_map/ppermute | solution.py:21
  45.0 0.0 collective-permute-done.4
  45.0 6.5 %scatter_fusion = pred[8,16]{1,0:T(8,128)(4,1)S(1)} fusion(pred[8,16]{1,0:T(8,128)(4,1)S(1)} %broadcast.176, s32[128]{0:T(128)S(1)} %fusion.18, pred[128]{0:T(512)(128)(4,1)S(1)} %broadcast.236), kind=kCustom, calls=%fused_computation.3 | custom fusion | bytes 1408 | tf_op jit(solution)/shard_map/scatter | solution.py:74
  51.5 0.2 dynamic_update_slice.25
  51.8 0.2 dynamic_update_slice.26
  52.0 0.2 dynamic_update_slice.27
  52.2 0.2 dynamic_update_slice.28
  52.4 0.2 dynamic_update_slice.29
  52.6 0.0 collective-permute-done.5
  52.6 0.2 dynamic_update_slice.30
  52.8 0.0 collective-permute-done.6
  52.8 0.2 dynamic_update_slice.31
  53.0 0.3 copy.12
  53.3 23.3 %fusion.23 = s32[8,128,1]{2,0,1:T(8,128)S(1)} fusion(s32[8,128,1]{2,0,1:T(8,128)S(1)} %copy.12), kind=kOutput, calls=%fused_computation.69 | output fusion | flops 130048 | bytes 8192 | tf_op jit(solution)/shard_map/jit(cumsum)/reduce_window_sum | solution.py:44
  76.6 0.3 copy.13
  76.9 0.1 compare_select_fusion
  77.0 0.2 copy.14
  77.3 0.1 multiply_reduce_fusion
  77.3 0.1 copy.19
  77.5 0.1 and_reduce_fusion
  77.5 0.1 copy.18
  77.7 4.3 %scatter_custom_fusion.4 = s32[128]{0:T(128)S(1)} fusion(s32[1024]{0:T(1024)S(1)} %bitcast.32, s32[1024]{0:T(1024)S(1)} %fusion.6, s32[]{:T(128)} %constant.145.clone.1), kind=kCustom, calls=%fused_computation.66 | custom fusion | bytes 516
  82.1 0.1 reshape.189
  82.1 4.5 %scatter_custom_fusion.3 = pred[128]{0:T(512)(128)(4,1)S(1)} fusion(s32[1024]{0:T(1024)S(1)} %bitcast.33, pred[1024]{0:T(1024)(128)(4,1)S(1)} %broadcast.235, pred[]{:T(512)} %constant.146.clone.1), kind=kCustom, calls=%fused_computation.56 | custom fusion | bytes 129
  86.7 0.1 reshape.185
  86.8 0.0 copy-start
  86.8 6.6 %gather_fusion = bf16[128,3584]{1,0:T(8,128)(2,1)S(1)} fusion(bf16[1188,3584]{1,0:T(8,128)(2,1)} %param.6, s32[1024]{0:T(1024)S(1)} %pad_clamp_fusion.2), kind=kCustom, calls=%fused_computation.2 | custom fusion | bytes 1835520 | tf_op jit(solution)/shard_map/jit(_take)/gather | solution.py:53
  93.4 1.1 select_select_fusion
  94.5 6.0 %all-to-all-start = ((bf16[8,16,3584]{2,1,0:T(8,128)(2,1)}), bf16[8,16,3584]{2,1,0:T(8,128)(2,1)S(1)}, u32[]{:S(2)}, u32[]{:S(2)}) async-start(bf16[8,16,3584]{2,1,0:T(8,128)(2,1)} %select_select_fusion), calls=%async_computation | async-start | bytes 1835008 | tf_op jit(solution)/shard_map/all_to_all | solution.py:55
  100.5 0.1 broadcast_select_fusion
  100.6 1.1 broadcast_select_fusion.1
  101.7 20.5 %all-to-all-done = bf16[8,16,3584]{2,1,0:T(8,128)(2,1)S(1)} async-done(((bf16[8,16,3584]{2,1,0:T(8,128)(2,1)}), bf16[8,16,3584]{2,1,0:T(8,128)(2,1)S(1)}, u32[]{:S(2)}, u32[]{:S(2)}) %all-to-all-start) | async-done | bytes 917536 | tf_op jit(solution)/shard_map/all_to_all | solution.py:55
  122.2 3.6 %all-to-all-start.1 = ((bf16[8,16,3584]{2,1,0:T(8,128)(2,1)}), bf16[8,16,3584]{2,1,0:T(8,128)(2,1)S(1)}, u32[]{:S(2)}, u32[]{:S(2)}) async-start(bf16[8,16,3584]{2,1,0:T(8,128)(2,1)} %broadcast_select_fusion.1), calls=%async_computation.1 | async-start | bytes 1835008 | tf_op jit(solution)/shard_map/all_to_all | solution.py:80
  125.7 0.0 all-reduce.2.cloned.1.call-start
  125.8 1.1 gather_fusion.1
  127.0 1.3 select_convert_fusion
  128.2 0.0 all-reduce.2.cloned.1.call-update
  128.3 0.1 reshape.179
  128.4 20.3 %all-to-all-done.1 = bf16[8,16,3584]{2,1,0:T(8,128)(2,1)S(1)} async-done(((bf16[8,16,3584]{2,1,0:T(8,128)(2,1)}), bf16[8,16,3584]{2,1,0:T(8,128)(2,1)S(1)}, u32[]{:S(2)}, u32[]{:S(2)}) %all-to-all-start.1) | async-done | bytes 917536 | tf_op jit(solution)/shard_map/all_to_all | solution.py:80
  148.6 10.0 %scatter_custom_fusion.2 = f32[1188,3584]{1,0:T(8,128)} fusion(s32[128]{0:T(128)S(1)} %fusion.16, f32[]{:T(128)} %constant.166.clone.1, bf16[128,3584]{1,0:T(8,128)(2,1)S(1)} %bitcast.31), kind=kCustom, calls=%fused_computation.8 | custom fusion | flops 917504 | bytes 17948676 | tf_op jit(solution)/shard_map/scatter-add | solution.py:85
  158.7 9.1 %convert_element_type.32 = bf16[1188,3584]{1,0:T(8,128)(2,1)} convert(f32[1188,3584]{1,0:T(8,128)} %scatter_custom_fusion.2) | non-fusion elementwise | flops 4257792 | bytes 25546752 | tf_op jit(solution)/shard_map/convert_element_type | solution.py:88
  167.8 2.2 %copy.31 = bf16[128,3584]{1,0:T(8,128)(2,1)} copy(bf16[128,3584]{1,0:T(8,128)(2,1)} %all-reduce.2.cloned.1.call-done) | data formatting | bytes 1835008
  (26 shorter events, 0.2 us)
Async XLA Ops:
  7.2 70.1 %copy-start.2 = (s32[2]{0:T(128)S(1)}, s32[2]{0:T(128)}, u32[]{:S(2)}) copy-start(s32[2]{0:T(128)} %constant.167) | copy-start | bytes 28
  7.2 70.3 %copy-start.1 = (s32[2]{0:T(128)S(1)}, s32[2]{0:T(128)}, u32[]{:S(2)}) copy-start(s32[2]{0:T(128)} %constant.170) | copy-start | bytes 28
  7.2 24.8 %collective-permute-start = (s32[128]{0:T(128)}, s32[128]{0:T(128)S(1)}, u32[]{:S(2)}, u32[]{:S(2)}) collective-permute-start(s32[128]{0:T(128)} %param.5), channel_id=1, source_target_pairs={{0,1},{1,2},{2,3},{3,4},{4,5},{5,6},{6,7},{7,0},{8,9},{9,10},{10,1... | collective-permute-start | bytes 1544 | tf_op jit(solution)/shard_map/ppermute | solution.py:18
  10.2 21.8 %collective-permute-start.1 = (s32[128]{0:T(128)}, s32[128]{0:T(128)S(1)}, u32[]{:S(2)}, u32[]{:S(2)}) collective-permute-start(s32[128]{0:T(128)} %param.5), channel_id=1, source_target_pairs={{0,7},{1,0},{2,1},{3,2},{4,3},{5,4},{6,5},{7,6},{8,15},{9,8},{10,9... | collective-permute-start | bytes 1544 | tf_op jit(solution)/shard_map/ppermute | solution.py:21
  32.0 6.3 %collective-permute-start.2 = (s32[128]{0:T(128)S(1)}, s32[128]{0:T(128)S(1)}, u32[]{:S(2)}, u32[]{:S(2)}) collective-permute-start(s32[128]{0:T(128)S(1)} %collective-permute-done), channel_id=1, source_target_pairs={{0,1},{1,2},{2,3},{3,4},{4,5},{5,6},{6,7},{7,0},{8,9},{9,10},{10,1... | collective-permute-start | bytes 1544 | tf_op jit(solution)/shard_map/ppermute | solution.py:18
  32.0 8.2 %collective-permute-start.3 = (s32[128]{0:T(128)S(1)}, s32[128]{0:T(128)S(1)}, u32[]{:S(2)}, u32[]{:S(2)}) collective-permute-start(s32[128]{0:T(128)S(1)} %collective-permute-done.1), channel_id=1, source_target_pairs={{0,7},{1,0},{2,1},{3,2},{4,3},{5,4},{6,5},{7,6},{8,15},{9,8},{10,9... | collective-permute-start | bytes 1544 | tf_op jit(solution)/shard_map/ppermute | solution.py:21
  38.3 6.7 %collective-permute-start.4 = (s32[128]{0:T(128)S(1)}, s32[128]{0:T(128)S(1)}, u32[]{:S(2)}, u32[]{:S(2)}) collective-permute-start(s32[128]{0:T(128)S(1)} %collective-permute-done.2), channel_id=1, source_target_pairs={{0,1},{1,2},{2,3},{3,4},{4,5},{5,6},{6,7},{7,0},{8,9},{9,10},{10,1... | collective-permute-start | bytes 1544 | tf_op jit(solution)/shard_map/ppermute | solution.py:18
  40.2 12.3 %collective-permute-start.5 = (s32[128]{0:T(128)S(1)}, s32[128]{0:T(128)S(1)}, u32[]{:S(2)}, u32[]{:S(2)}) collective-permute-start(s32[128]{0:T(128)S(1)} %collective-permute-done.3), channel_id=1, source_target_pairs={{0,7},{1,0},{2,1},{3,2},{4,3},{5,4},{6,5},{7,6},{8,15},{9,8},{10,9... | collective-permute-start | bytes 1544 | tf_op jit(solution)/shard_map/ppermute | solution.py:21
  45.0 7.8 %collective-permute-start.6 = (s32[128]{0:T(128)S(1)}, s32[128]{0:T(128)S(1)}, u32[]{:S(2)}, u32[]{:S(2)}) collective-permute-start(s32[128]{0:T(128)S(1)} %collective-permute-done.4), channel_id=1, source_target_pairs={{0,1},{1,2},{2,3},{3,4},{4,5},{5,6},{6,7},{7,0},{8,9},{9,10},{10,1... | collective-permute-start | bytes 1544 | tf_op jit(solution)/shard_map/ppermute | solution.py:18
  86.8 39.0 %copy-start = (s32[128]{0:T(128)S(1)}, s32[128]{0:T(128)}, u32[]{:S(2)}) copy-start(s32[128]{0:T(128)} %param.5) | copy-start | bytes 1540
  94.5 27.7 %all-to-all-start = ((bf16[8,16,3584]{2,1,0:T(8,128)(2,1)}), bf16[8,16,3584]{2,1,0:T(8,128)(2,1)S(1)}, u32[]{:S(2)}, u32[]{:S(2)}) async-start(bf16[8,16,3584]{2,1,0:T(8,128)(2,1)} %select_select_fusion), calls=%async_computation | async-start | bytes 1835008 | tf_op jit(solution)/shard_map/all_to_all | solution.py:55
  122.2 26.4 %all-to-all-start.1 = ((bf16[8,16,3584]{2,1,0:T(8,128)(2,1)}), bf16[8,16,3584]{2,1,0:T(8,128)(2,1)S(1)}, u32[]{:S(2)}, u32[]{:S(2)}) async-start(bf16[8,16,3584]{2,1,0:T(8,128)(2,1)} %broadcast_select_fusion.1), calls=%async_computation.1 | async-start | bytes 1835008 | tf_op jit(solution)/shard_map/all_to_all | solution.py:80
  125.7 42.0 %all-reduce.2.cloned.1.call-start = ((), (), s32[]{:S(2)}) async-start(), calls=%async_computation.2 | async-start | bytes 1835008 | tf_op jit(solution)/shard_map/psum | solution.py:87
Sparse Core Ops, SparseCore 0:
  129.5 36.2 all-reduce.1
